TPU v7x, 32 devices: a whole 2x2x4 slice. The times are simulated.
32 devices in a mesh: col: 32 (over z, y, x, core).
Axes of the slice: x: 2, y: 2, z: 4, core: 2. Of those that a mesh axis runs over, the one named last changes fastest.
Arguments:
- matrix: float32 [4096, 4096], P(None, 'col'), as said below
- rhs_rows: float32 [2048, 4096], P('col'), may hold values from -6 to 6
Outputs:
- eliminated: float32 [4096, 4096], P(None, 'col')
- solved_rows: float32 [2048, 4096], P('col')
Inputs may be any that keep to these rules, and one draw needn't show every extreme that they name: `matrix`: the diagonal entries lie between 1.5 * sqrt(4096) and 3 * sqrt(4096); the other entries between -4 and 4.
All inputs are finite; a program needn't handle non-finite values.
Results may differ from a plain program's by a relative error of at most 0.0001.
Values sent between devices are 32-bit elements; how exact they have to be, the bound alone decides.
No kernel may reach another device: no remote copies, remote signals or barrier semaphores. Data moves between devices by JAX's collectives and lax.ppermute only.
A program may use at most 192 MiB of HBM per device.

v0:
```python
import jax
import jax.numpy as jnp
from jax import lax
from jax.sharding import PartitionSpec as P

BLK = 128
BLK_DEV = 1
STEPS = 2


def broadcast(value, axis, source):
    kept = jnp.where(lax.axis_index(axis) == source, value, 0).astype(value.dtype)
    return lax.psum(kept, axis)


def pivot_inverse(pivot_block):
    gram = jnp.dot(
        pivot_block.T,
        pivot_block,
        precision=lax.Precision.HIGHEST,
        preferred_element_type=jnp.float32,
    )
    lower = jnp.linalg.cholesky(gram)
    return jax.scipy.linalg.cho_solve((lower, True), pivot_block.T)


def unchanged(local_cols):
    return local_cols


def body(matrix, rhs_rows):
    precise = lax.Precision.HIGHEST
    own_index = lax.axis_index("col")
    fetched = []
    for step in range(STEPS):
        fetched.append(broadcast(matrix, "col", step))
    for step in range(STEPS):
        row_start = step * BLK_DEV * BLK
        row_end = row_start + BLK
        panel_cols = fetched[step]
        inverse = pivot_inverse(panel_cols[row_start:row_end])
        scaled = jnp.dot(
            inverse,
            matrix[row_start:row_end],
            precision=precise,
            preferred_element_type=jnp.float32,
        )
        matrix = matrix - jnp.dot(
            panel_cols, scaled, precision=precise, preferred_element_type=jnp.float32
        )
        matrix = matrix.at[row_start:row_end].set(scaled)

        def place_column(local_cols):
            column = -jnp.dot(
                panel_cols, inverse, precision=precise, preferred_element_type=jnp.float32
            )
            column = column.at[row_start:row_end].set(inverse)
            return local_cols.at[:, :BLK].set(column)

        matrix = lax.cond(own_index == step, place_column, unchanged, matrix)
        solved = jnp.dot(
            rhs_rows[:, row_start:row_end],
            inverse.T,
            precision=precise,
            preferred_element_type=jnp.float32,
        )
        rhs_rows = rhs_rows - jnp.dot(
            solved, panel_cols.T, precision=precise, preferred_element_type=jnp.float32
        )
        rhs_rows = rhs_rows.at[:, row_start:row_end].set(solved)
        for later in range(step + 1, STEPS):
            row_part = jnp.dot(
                inverse,
                fetched[later][row_start:row_end],
                precision=precise,
                preferred_element_type=jnp.float32,
            )
            updated = fetched[later] - jnp.dot(
                panel_cols, row_part, precision=precise, preferred_element_type=jnp.float32
            )
            fetched[later] = updated.at[row_start:row_end].set(row_part)
    return (matrix, rhs_rows)


def solution(mesh):
    return jax.shard_map(
        body,
        mesh=mesh,
        in_specs=(P(None, "col"), P("col", None)),
        out_specs=(P(None, "col"), P("col", None)),
        check_vma=False,
    )
```

profile of v0, /device:TPU:0, one launch (start us, length us, event | category | flops | bytes accessed | tf_op | source)
XLA Modules:
  0.0 248.9 jit_solution(937625850335362420)
XLA Ops:
  7.2 3.9 %broadcast_select_fusion = (f32[4096,128]{1,0:T(8,128)}, f32[4096,128]{1,0:T(8,128)}) fusion(f32[4096,128]{1,0:T(8,128)} %param.31, pred[]{:T(512)S(6)} %eq.8, pred[]{:T(512)S(6)} %eq.9), kind=kLoop, calls=%fused_computation.7 | loop fusion | flops 1048576 | bytes 6291458 | tf_op jit(solution)/shard_map/jit(_where)/select_n | solution.py:12
  11.1 0.7 compare_reduce_fusion.3
  11.8 0.7 compare_reduce_fusion.2
  12.5 147.2 %all-reduce.3.cloned.1.call-done = (f32[4096,128]{1,0:T(8,128)}, f32[4096,128]{1,0:T(8,128)}) async-done(((f32[4096,128]{1,0:T(8,128)}, f32[4096,128]{1,0:T(8,128)}), (f32[4096,128]{1,0:T(8,128)}, f32[4096,128]{1,0:T(8,128)})) %all-reduce.3.cloned.1.call-update) | async-done | bytes 4194320 | tf_op jit(solution)/shard_map/psum | solution.py:13
  159.7 1.2 fusion.24
  161.0 11.7 %cholesky.44 = f32[128,128]{1,0:T(8,128)S(1)} custom-call(f32[128,128]{1,0:T(8,128)S(1)} %fusion.17), custom_call_target="Cholesky" | custom-call | tf_op jit(solution)/shard_map/jit(cholesky)/cholesky | solution.py:23
  172.7 0.6 compare_reduce_fusion.1
  173.4 0.7 fusion
  174.1 9.8 %custom-call.8 = f32[1,128,128]{1,2,0:T(8,128)S(1)} custom-call(f32[1,128,128]{2,1,0:T(8,128)S(1)} %fusion), custom_call_target="InvertDiagBlocksLowerTriangular" | custom-call | tf_op jit(solution)/shard_map/jit(_cho_solve)/triangular_solve | solution.py:24
  183.9 1.1 fusion.12
  185.2 1.0 fusion.18
  186.5 1.0 fusion.4
  187.6 4.2 %convolution_subtract_fusion = f32[4096,128]{1,0:T(8,128)S(1)} fusion(f32[4096,128]{1,0:T(8,128)} %get-tuple-element.213, f32[4096,128]{1,0:T(8,128)} %get-tuple-element.212, f32[128,128]{1,0:T(8,128)S(1)} %fusion.4), kind=kOutput, calls=%fused_computation.4 | convolution fusion | flops 805830656 | bytes 6356992 | tf_op jit(solution)/shard_map/dot_general | solution.py:78
  191.8 1.3 copy-done.1
  193.6 11.8 %cholesky.55 = f32[128,128]{1,0:T(8,128)S(1)} custom-call(f32[128,128]{1,0:T(8,128)S(1)} %fusion.11), custom_call_target="Cholesky" | custom-call | tf_op jit(solution)/shard_map/jit(cholesky)/cholesky | solution.py:23
  205.4 0.6 compare_reduce_fusion
  206.1 0.6 fusion.1
  206.7 9.8 %custom-call.9 = f32[1,128,128]{1,2,0:T(8,128)S(1)} custom-call(f32[1,128,128]{2,1,0:T(8,128)S(1)} %fusion.1), custom_call_target="InvertDiagBlocksLowerTriangular" | custom-call | tf_op jit(solution)/shard_map/jit(_cho_solve)/triangular_solve | solution.py:24
  216.5 1.1 fusion.6
  217.9 2.4 convolution_subtract_fusion.2
  220.3 0.6 fusion.29
  221.2 2.4 convolution_subtract_fusion.1
  223.6 1.8 fusion.32
  225.5 3.7 %conditional.2 = (f32[4096,128]{1,0:T(8,128)}) conditional(s32[]{:T(128)} %convert_element_type.10, (f32[4096,128]{1,0:T(8,128)S(1)}, f32[4096,128]{1,0:T(8,128)S(1)}, f32[128,128]{1,0:T(8,128)S(1)}) %tuple.107, (f32[4096,128]{1,0:T(8,128)S(1)}, f32[128,128]{1,0:T(8,128)S(1)}) %tuple.105), branch_computations={%region_3.6_spmd, %region_4.7_spmd} | conditional | flops 805830656 | bytes 6422536 | solution.py:60
  225.5 3.1 %convolution_negate_fusion = f32[4096,128]{1,0:T(8,128)} fusion(f32[4096,128]{1,0:T(8,128)S(1)} %get-tuple-element.197, f32[128,128]{1,0:T(8,128)S(1)} %get-tuple-element.198), kind=kOutput, calls=%fused_computation.1 | convolution fusion | flops 805830656 | bytes 4259840 | tf_op jit(solution)/shard_map/cond/branch_1_fun/dot_general | solution.py:54
  229.2 1.0 fusion.2
  230.3 4.9 %fusion.33 = f32[4096,128]{1,0:T(8,128)} fusion(f32[4096,128]{1,0:T(8,128)} %copy-done.1, f32[128,128]{1,0:T(8,128)S(1)} %fusion.2), kind=kOutput, calls=%fused_computation.58 | convolution fusion | flops 805306368 | bytes 4259840 | tf_op jit(solution)/shard_map/dot_general | solution.py:48
  235.1 0.6 fusion.26
  235.8 1.0 copy-done.6
  236.8 3.8 %conditional.3 = (f32[4096,128]{1,0:T(8,128)}, f32[128,128]{1,0:T(8,128)S(1)}, s32[]{:T(128)}) conditional(s32[]{:T(128)} %convert_element_type.9, (f32[4096,128]{1,0:T(8,128)}, f32[4096,128]{1,0:T(8,128)}, f32[128,128]{1,0:T(8,128)S(1)}) %tuple.94, (f32[4096,128]{1,0:T(8,128)S(1)}, f32[128,128]{1,0:T(8,128)S(1)}) %tuple.106), branch_computations={%region_6.0_spmd, %region_7.10_spmd} | conditional | flops 805830656 | bytes 6291488 | solution.py:60
  236.8 3.8 %sub.15 = f32[4096,128]{1,0:T(8,128)} subtract(f32[4096,128]{1,0:T(8,128)} %get-tuple-element.199, f32[4096,128]{1,0:T(8,128)} %get-tuple-element.200) | non-fusion elementwise | flops 524288 | bytes 6291456 | tf_op jit(solution)/shard_map/sub | solution.py:48
  240.5 1.5 scatter.30
  (27 shorter events, 2.2 us)
Async XLA Ops:
  7.2 152.5 %all-reduce.3.cloned.1.call-start = ((), (), s32[]{:S(2)}) async-start(), calls=%async_computation | async-start | bytes 8388608 | tf_op jit(solution)/shard_map/psum | solution.py:13
  11.1 175.2 %copy-start.5 = (f32[64,4096]{1,0:T(8,128)S(1)}, f32[64,4096]{1,0:T(8,128)}, u32[]{:S(2)}) copy-start(f32[64,4096]{1,0:T(8,128)} %param.32) | copy-start | bytes 3145732
  187.6 30.3 %copy-start = (f32[4096,128]{1,0:T(8,128)S(1)}, f32[4096,128]{1,0:T(8,128)}, u32[]{:S(2)}) copy-start(f32[4096,128]{1,0:T(8,128)} %get-tuple-element.212) | copy-start | bytes 6291460
  191.8 1.3 copy-start.1
  217.9 3.3 %copy-start.2 = (f32[4096,128]{1,0:T(8,128)S(1)}, f32[4096,128]{1,0:T(8,128)}, u32[]{:S(2)}) copy-start(f32[4096,128]{1,0:T(8,128)} %copy-done.1) | copy-start | bytes 6291460
  223.6 1.9 copy-start.4
  230.2 4.9 %copy-start.3 = (f32[4096,128]{1,0:T(8,128)S(1)}, f32[4096,128]{1,0:T(8,128)}, u32[]{:S(2)}) copy-start(f32[4096,128]{1,0:T(8,128)} %copy-done.1) | copy-start | bytes 6291460
  235.8 1.0 copy-start.6
Sparse Core Ops, SparseCore 0:
  14.3 145.3 all-reduce.2
where the time goes:
time: 249 us
  waiting for transfers between devices  147 us (59%)
  other arithmetic  56.1 us (23%)
  matrix products  26.6 us (11%)
  between operations  14.3 us (6%)
  local copies, waits for them, and re-layouts  4.64 us (2%)
    psum x1, waiting for transfers between devices, broadcast(): return lax.psum(kept, axis)  147 us
    another operation x6, other arithmetic, pivot_inverse(): lower = jnp.linalg.cholesky(gram)  24.9 us
    another operation x4, other arithmetic, pivot_inverse(): return jax.scipy.linalg.cho_solve((lower, True), pivot_block.T)  20.9 us
    dot_general x2, matrix products, body(): jnp.dot(panel_cols, scaled, precision=precise, preferred_element_type=jnp...  6.72 us
  transfers between devices with their start and end apart: 1, of which 1 were waited for; matrix products, arithmetic and copies ran while one was open for 1% of the time, Pallas kernels for 0%

commit v1 on v0

--- a/solution.py
+++ b/solution.py
@@ -8,9 +8,15 @@
 STEPS = 2
 
 
+def add_all(x, axis):
+    parts = lax.all_gather(x, axis, axis=0, tiled=False)
+    summed = parts.sum(axis=0)
+    return summed
+
+
 def broadcast(value, axis, source):
     kept = jnp.where(lax.axis_index(axis) == source, value, 0).astype(value.dtype)
-    return lax.psum(kept, axis)
+    return add_all(kept, axis)
 
 
 def pivot_inverse(pivot_block):

time: 249 us -> 812 us (3.26)
  waiting for transfers between devices: 147 us -> 667 us
  other arithmetic: 56.1 us -> 101 us
    all_gather x0 -> x2, waiting for transfers between devices: none -> 666 us  [add_all(): parts = lax.all_gather(x, axis, axis=0, tiled=False)]
    psum x1 -> x0, waiting for transfers between devices: 147 us -> none  [broadcast(): return lax.psum(kept, axis)]
    reduce_sum x0 -> x2, other arithmetic: none -> 45.3 us  [add_all(): summed = parts.sum(axis=0)]
  transfers between devices with their start and end apart: 1 -> 2, of which waited for: 1 -> 2; matrix products, arithmetic and copies ran while one was open for 1% -> 6% of each run, Pallas kernels for 0% -> 0%
where the time goes in v1:
time: 812 us; the launch traced here: 811 us
  waiting for transfers between devices  667 us (82%)
  other arithmetic  101 us (12%)
  matrix products  24.3 us (3%)
  between operations  14.3 us (2%)
    all_gather x2, waiting for transfers between devices, add_all(): parts = lax.all_gather(x, axis, axis=0, tiled=False)  666 us
    reduce_sum x2, other arithmetic, add_all(): summed = parts.sum(axis=0)  45.3 us
    another operation x6, other arithmetic, pivot_inverse(): lower = jnp.linalg.cholesky(gram)  24.8 us
    another operation x4, other arithmetic, pivot_inverse(): return jax.scipy.linalg.cho_solve((lower, True), pivot_block.T)  20.9 us
  transfers between devices with their start and end apart: 2, of which 2 were waited for; matrix products, arithmetic and copies ran while one was open for 6% of the time, Pallas kernels for 0%

profile of v1, /device:TPU:0, one launch (start us, length us, event | category | flops | bytes accessed | tf_op | source)
XLA Modules:
  0.0 811.3 jit_solution(13815869645695718542)
XLA Ops:
  7.2 3.9 broadcast_select_fusion
  11.2 0.7 all-gather.7.cloned.1.call-update
  11.9 0.6 compare_reduce_fusion.3
  12.5 0.7 compare_reduce_fusion.2
  13.2 356.5 %all-gather.5.cloned.1.call-done = f32[131072,128]{1,0:T(8,128)} async-done(((f32[4096,128]{1,0:T(8,128)}), f32[131072,128]{1,0:T(8,128)}) %all-gather.5.cloned.1.call-update) | async-done | bytes 67108880 | tf_op jit(solution)/shard_map/all_gather | solution.py:12
  369.7 23.0 %reduce_sum.18 = f32[4096,128]{1,0:T(8,128)S(1)} reduce(f32[32,4096,128]{2,1,0:T(8,128)} %bitcast, f32[]{:T(128)} %constant.313.clone.1), dimensions={0}, to_apply=%region_0.1 | reduce | flops 16252928 | bytes 69206016 | tf_op jit(solution)/shard_map/reduce_sum | solution.py:13
  393.1 11.7 %cholesky.44 = f32[128,128]{1,0:T(8,128)S(1)} custom-call(f32[128,128]{1,0:T(8,128)S(1)} %fusion.17), custom_call_target="Cholesky" | custom-call | tf_op jit(solution)/shard_map/jit(cholesky)/cholesky | solution.py:29
  404.8 0.6 compare_reduce_fusion.1
  406.0 9.8 %custom-call.8 = f32[1,128,128]{1,2,0:T(8,128)S(1)} custom-call(f32[1,128,128]{2,1,0:T(8,128)S(1)} %fusion), custom_call_target="InvertDiagBlocksLowerTriangular" | custom-call | tf_op jit(solution)/shard_map/jit(_cho_solve)/triangular_solve | solution.py:30
  416.3 1.0 fusion.18
  417.4 309.6 %all-gather.7.cloned.1.call-done = f32[131072,128]{1,0:T(8,128)} async-done(((f32[4096,128]{1,0:T(8,128)}), f32[131072,128]{1,0:T(8,128)}) %all-gather.7.cloned.1.call-update) | async-done | bytes 67108880 | tf_op jit(solution)/shard_map/all_gather | solution.py:12
  727.0 22.3 %reduce_sum.19 = f32[4096,128]{1,0:T(8,128)} reduce(f32[32,4096,128]{2,1,0:T(8,128)} %bitcast.5, f32[]{:T(128)} %constant.313.clone.1), dimensions={0}, to_apply=%region_5.0 | reduce | flops 16252928 | bytes 69206016 | tf_op jit(solution)/shard_map/reduce_sum | solution.py:13
  749.6 1.0 fusion.4
  750.6 3.5 convolution_subtract_fusion
  754.1 1.3 copy-done
  755.8 11.7 %cholesky.55 = f32[128,128]{1,0:T(8,128)S(1)} custom-call(f32[128,128]{1,0:T(8,128)S(1)} %fusion.11), custom_call_target="Cholesky" | custom-call | tf_op jit(solution)/shard_map/jit(cholesky)/cholesky | solution.py:29
  767.6 0.7 compare_reduce_fusion
  768.3 0.7 fusion.1
  769.0 9.8 %custom-call.9 = f32[1,128,128]{1,2,0:T(8,128)S(1)} custom-call(f32[1,128,128]{2,1,0:T(8,128)S(1)} %fusion.1), custom_call_target="InvertDiagBlocksLowerTriangular" | custom-call | tf_op jit(solution)/shard_map/jit(_cho_solve)/triangular_solve | solution.py:30
  778.8 1.1 fusion.6
  780.2 2.4 convolution_subtract_fusion.2
  783.4 2.6 convolution_subtract_fusion.1
  786.0 1.8 fusion.32
  787.9 3.7 conditional.2
  787.9 3.1 convolution_negate_fusion
  791.6 1.0 fusion.2
  792.7 4.9 fusion.33
  797.6 0.6 fusion.26
  798.2 1.0 copy-done.5
  799.2 3.8 conditional.3
  799.2 3.8 sub.15
  802.9 1.5 scatter.30
  (30 shorter events, 3.9 us)
Async XLA Ops:
  7.2 362.5 %all-gather.5.cloned.1.call-start = ((), (), s32[]{:S(2)}) async-start(), calls=%async_computation | async-start | bytes 69206016 | tf_op jit(solution)/shard_map/all_gather | solution.py:12
  11.1 715.8 %all-gather.7.cloned.1.call-start = ((), (), s32[]{:S(2)}) async-start(), calls=%async_computation.1 | async-start | bytes 69206016 | tf_op jit(solution)/shard_map/all_gather | solution.py:12
  727.0 22.4 %copy-start.4 = (f32[64,4096]{1,0:T(8,128)S(1)}, f32[64,4096]{1,0:T(8,128)}, u32[]{:S(2)}) copy-start(f32[64,4096]{1,0:T(8,128)} %param.32) | copy-start | bytes 3145732
  754.1 1.3 copy-start
  780.2 3.2 copy-start.1
  786.0 1.9 copy-start.3
  792.7 4.9 copy-start.2
  798.2 1.0 copy-start.5
Sparse Core Ops, SparseCore 0:
  11.3 358.3 all-gather.4
  373.1 353.8 all-gather.6
